TPU v7x, 32 devices: a whole 2x2x4 slice. The times are simulated.
32 devices in a mesh: prow: 4 (over y, core), pcol: 8 (over z, x).
Axes of the slice: x: 2, y: 2, z: 4, core: 2. Of those that a mesh axis runs over, the one named last changes fastest.
Arguments:
- vectors: bfloat16 [512, 120064], P('pcol', 'prow'), may hold values from -6 to 6
- reflectors: bfloat16 [2, 256, 120064], P(None, 'pcol', 'prow'), may hold values from -6 to 6
- panel_factor: float32 [2, 256, 256], replicated, as said below
Outputs:
- band_vectors: bfloat16 [8, 64, 120064], P('pcol', 'prow')
Inputs may be any that keep to these rules, and one draw needn't show every extreme that they name: `panel_factor`: upper triangular: zero below the diagonal; diagonal entries between 1 / 120064 and 3 / 120064.
All inputs are finite; a program needn't handle non-finite values.
Results may differ from a plain program's by a relative error of at most 0.0095.
Values may be sent and summed in bfloat16 or wider, within the bound.
A program may use at most 192 MiB of HBM per device.

v0:
```python
import jax
import jax.numpy as jnp
from jax import lax
from jax.sharding import PartitionSpec as P


def finish_panel(current, panel, factor, projected):
    scaled = lax.dot_general(
        projected,
        factor,
        (((1,), (1,)), ((), ())),
        precision=lax.Precision.HIGHEST,
        preferred_element_type=jnp.float32,
    ).astype(jnp.bfloat16)
    updated = current.astype(jnp.float32) - jnp.dot(
        scaled, panel, preferred_element_type=jnp.float32
    )
    return updated.astype(jnp.bfloat16)


def partial_products(current, panel):
    return lax.dot_general(
        current, panel, (((1,), (1,)), ((), ())), preferred_element_type=jnp.float32
    )


def apply_panel(current, panel, factor):
    partial_sum = partial_products(current, panel)
    projected = lax.psum(partial_sum.astype(jnp.bfloat16), "prow").astype(jnp.float32)
    return finish_panel(current, panel, factor, projected)


def body(vectors, reflectors, panel_factor):
    current = vectors
    for number in range(reflectors.shape[0]):
        single = lax.all_gather(reflectors[number], "pcol", axis=0, tiled=True)
        current = apply_panel(current, single, panel_factor[number])
    owned_rows = lax.all_to_all(current, "prow", split_axis=0, concat_axis=1, tiled=True)
    return owned_rows[None]


def solution(mesh):
    placed = (P("pcol", "prow"), P(None, "pcol", "prow"), P())
    return jax.shard_map(
        body, mesh=mesh, in_specs=placed, out_specs=P("pcol", "prow", None), check_vma=False
    )
```

profile of v0, /device:TPU:0, one launch (start us, length us, event | category | flops | bytes accessed | tf_op | source)
XLA Modules:
  0.0 529.0 jit_solution(264437417981960315)
XLA Ops:
  6.5 0.0 all-gather.5.cloned.1.call-start
  6.5 4.2 fusion.18
  10.8 0.0 all-gather.5.cloned.1.call-update
  10.8 0.0 all-gather.7.cloned.1.call-start
  10.9 0.7 all-gather.7.cloned.1.call-update
  11.6 0.0 copy-start
  11.6 212.6 %all-gather.5.cloned.1.call-done = bf16[1,256,30016]{2,1,0:T(8,128)(2,1)} async-done(((bf16[1,32,30016]{2,1,0:T(8,128)(2,1)}), bf16[1,256,30016]{2,1,0:T(8,128)(2,1)}) %all-gather.5.cloned.1.call-update) | async-done | bytes 15368208 | tf_op jit(solution)/shard_map/all_gather | solution.py:36
  224.2 11.2 %fusion.8 = bf16[64,256]{1,0:T(8,128)(2,1)S(1)} fusion(bf16[64,30016]{1,0:T(8,128)(2,1)} %param.3, bf16[1,256,30016]{2,1,0:T(8,128)(2,1)} %all-gather.5.cloned.1.call-done), kind=kOutput, calls=%fused_computation.10 | convolution fusion | flops 983580672 | bytes 19243008 | tf_op jit(solution)/shard_map/dot_general | solution.py:22
  235.4 11.2 %psum.14 = bf16[64,256]{1,0:T(8,128)(2,1)S(1)} all-reduce(bf16[64,256]{1,0:T(8,128)(2,1)S(1)} %fusion.8), channel_id=1, replica_groups=mesh['prow'=4,'pcol'=8] {'prow'}, use_global_device_ids=true, to_apply=%region_0.0 | all-reduce | flops 16384 | bytes 65536 | tf_op jit(solution)/shard_map/psum | solution.py:29
  246.6 0.0 copy-done
  246.6 0.3 convolution_convert_fusion.1
  246.9 10.6 %fusion = bf16[64,30016]{1,0:T(8,128)(2,1)} fusion(bf16[64,256]{1,0:T(8,128)(2,1)S(1)} %convolution_convert_fusion.1, bf16[1,256,30016]{2,1,0:T(8,128)(2,1)} %all-gather.5.cloned.1.call-done, bf16[64,30016]{1,0:T(8,128)(2,1)} %param.3), kind=kOutput, calls=%fused_computation.2 | convolution fusion | flops 989327360 | bytes 23085056 | tf_op jit(solution)/shard_map/dot_general | solution.py:15
  257.5 177.6 %all-gather.7.cloned.1.call-done = bf16[1,256,30016]{2,1,0:T(8,128)(2,1)} async-done(((bf16[1,32,30016]{2,1,0:T(8,128)(2,1)}), bf16[1,256,30016]{2,1,0:T(8,128)(2,1)}) %all-gather.7.cloned.1.call-update) | async-done | bytes 15368208 | tf_op jit(solution)/shard_map/all_gather | solution.py:36
  435.0 11.2 %fusion.11 = bf16[64,256]{1,0:T(8,128)(2,1)S(1)} fusion(bf16[64,30016]{1,0:T(8,128)(2,1)} %fusion, bf16[1,256,30016]{2,1,0:T(8,128)(2,1)} %all-gather.7.cloned.1.call-done), kind=kOutput, calls=%fused_computation.11 | convolution fusion | flops 983580672 | bytes 19243008 | tf_op jit(solution)/shard_map/dot_general | solution.py:22
  446.3 10.4 %psum.15 = bf16[64,256]{1,0:T(8,128)(2,1)S(1)} all-reduce(bf16[64,256]{1,0:T(8,128)(2,1)S(1)} %fusion.11), channel_id=1, replica_groups=mesh['prow'=4,'pcol'=8] {'prow'}, use_global_device_ids=true, to_apply=%region_1.0 | all-reduce | flops 16384 | bytes 65536 | tf_op jit(solution)/shard_map/psum | solution.py:29
  456.6 0.3 convolution_convert_fusion
  456.9 8.7 %fusion.1 = bf16[64,30016]{1,0:T(8,128)(2,1)S(1)} fusion(bf16[64,256]{1,0:T(8,128)(2,1)S(1)} %convolution_convert_fusion, bf16[1,256,30016]{2,1,0:T(8,128)(2,1)} %all-gather.7.cloned.1.call-done, bf16[64,30016]{1,0:T(8,128)(2,1)} %fusion), kind=kOutput, calls=%fused_computation.3 | convolution fusion | flops 989327360 | bytes 23085056 | tf_op jit(solution)/shard_map/dot_general | solution.py:15
  465.6 47.1 %all_to_all.16 = bf16[4,16,30016]{2,1,0:T(8,128)(2,1)S(1)} all-to-all(bf16[4,16,30016]{2,1,0:T(8,128)(2,1)S(1)} %bitcast.28), channel_id=1, replica_groups=mesh['prow'=4,'pcol'=8] {'prow'}, dimensions={0} | all-to-all | bytes 7684096 | tf_op jit(solution)/shard_map/all_to_all | solution.py:38
  512.7 3.3 copy.4
  516.0 6.2 %broadcast_in_dim.3 = bf16[1,16,120064]{2,1,0:T(8,128)(2,1)} reshape(bf16[16,4,30016]{2,1,0:T(4,128)(2,1)} %copy.4) | data formatting | bytes 7684096 | tf_op jit(solution)/shard_map/broadcast_in_dim | solution.py:39
Async XLA Ops:
  6.5 217.6 %all-gather.5.cloned.1.call-start = ((), (), s32[]{:S(2)}) async-start(), calls=%async_computation.1 | async-start | bytes 17326080 | tf_op jit(solution)/shard_map/all_gather | solution.py:36
  10.8 424.2 %all-gather.7.cloned.1.call-start = ((), (), s32[]{:S(2)}) async-start(), calls=%async_computation.2 | async-start | bytes 17326080 | tf_op jit(solution)/shard_map/all_gather | solution.py:36
  11.6 235.0 %copy-start = (f32[2,256,256]{2,1,0:T(8,128)S(1)}, f32[2,256,256]{2,1,0:T(8,128)}, u32[]{:S(2)}) copy-start(f32[2,256,256]{2,1,0:T(8,128)} %param.5) | copy-start | bytes 1572868
Sparse Core Ops, SparseCore 0:
  10.9 213.1 all-gather.4
  226.3 208.6 all-gather.6
where the time goes:
time: 529 us
  waiting for transfers between devices  391 us (74%)
  blocking collectives  68.6 us (13%)
  matrix products  42.3 us (8%)
  local copies, waits for them, and re-layouts  13.8 us (3%)
  between operations  13.5 us (3%)
    all_gather x2, waiting for transfers between devices, body(): single = lax.all_gather(reflectors[number], 'pcol', axis=0, tiled=True)  390 us
    all_to_all x1, blocking collectives, body(): lax.all_to_all(current, 'prow', split_axis=0, concat_axis=1, tiled=True)  47.1 us
    dot_general x2, matrix products, partial_products(): lax.dot_general(current, panel, (((1,), (1,)), ((), ())), preferred_eleme...  22.5 us
    psum x2, blocking collectives, apply_panel(): lax.psum(partial_sum.astype(jnp.bfloat16), 'prow').astype(jnp.float32)  21.5 us
    dot_general x2, matrix products, finish_panel(): jnp.dot(scaled, panel, preferred_element_type=jnp.float32)  19.3 us
  transfers between devices with their start and end apart: 2, of which 2 were waited for; matrix products, arithmetic and copies ran while one was open for 4% of the time, Pallas kernels for 0%

commit v1 on v0

v1 whole, which is shorter than its diff:
```python
import functools

import jax
import jax.numpy as jnp
from jax import lax
from jax.experimental import pallas as pl
from jax.experimental.pallas import tpu as pltpu
from jax.sharding import PartitionSpec as P

MESH = pl.DeviceIdType.MESH
LANES = 128
SPLIT = 4
F32, BF16 = jnp.float32, jnp.bfloat16
NT = (((1,), (1,)), ((), ()))


def kernel(
    n_row, n_col, chunk, k_block, out_blocks,
    v_ref, w_ref, t_ref, o_ref,
    v_s, w_s, part, rs_send, rs_recv, ag, s_s,
    v_send, v_recv, w_send, w_recv, r_send, r_recv, g_send, g_recv, o_send, o_recv, l_sem,
):
    me_r, me_c = lax.axis_index("prow"), lax.axis_index("pcol")
    me_a, me_b = lax.rem(me_c, SPLIT), lax.div(me_c, SPLIT)
    halves, group = n_col // SPLIT, SPLIT * n_row
    me_g = me_a * n_row + me_r
    width = v_s.shape[2]
    rows = SPLIT * v_s.shape[1]
    panel = w_s.shape[1] * w_s.shape[2]
    own = v_s.shape[1] // n_row

    def remote(src, dst, send, recv, r, c):
        return pltpu.make_async_remote_copy(
            src_ref=src, dst_ref=dst, send_sem=send, recv_sem=recv,
            device_id={"prow": r, "pcol": c}, device_id_type=MESH,
        )

    def cut(ref_rows, q):
        return ref_rows.at[:, pl.ds(pl.multiple_of(q * chunk, LANES), chunk)]

    def cut_w(q):
        return w_ref.at[:, :, pl.ds(pl.multiple_of(q * chunk, LANES), chunk)]

    def slot_w(c):
        return w_s.at[:, c, :, pl.ds(0, chunk)]

    def slot_v(a):
        return v_s.at[a, :, pl.ds(0, chunk)]

    sends, arrivals, local = [], [], []
    for kb in reversed(range(halves)):
        b = lax.rem(me_b + kb, halves)
        for ka in reversed(range(SPLIT)):
            q = lax.rem(me_a + ka, SPLIT)
            c = b * SPLIT + q
            if ka or kb:
                copy = remote(cut_w(q), slot_w(me_c), w_send.at[c], w_recv.at[me_c], me_r, c)
                copy.start()
                sends.append(copy)
                arrivals.append(
                    remote(cut_w(q), slot_w(c), w_send.at[c], w_recv.at[c], me_r, c)
                )
            else:
                copy = pltpu.make_async_copy(cut_w(me_a), slot_w(me_c), l_sem.at[0])
                copy.start()
                local.append(copy)
            if kb == 0:
                if ka:
                    copy = remote(cut(v_ref, q), slot_v(me_a), v_send.at[q], v_recv.at[me_a], me_r, c)
                    copy.start()
                    sends.append(copy)
                    arrivals.append(
                        remote(cut(v_ref, q), slot_v(q), v_send.at[q], v_recv.at[q], me_r, c)
                    )
                else:
                    copy = pltpu.make_async_copy(cut(v_ref, me_a), slot_v(me_a), l_sem.at[1])
                    copy.start()
                    local.append(copy)
    if width > chunk:
        v_s[:, :, chunk:] = jnp.zeros((SPLIT, v_s.shape[1], width - chunk), BF16)
        w_s[:, :, :, chunk:] = jnp.zeros((2, n_col, w_s.shape[2], width - chunk), BF16)
    part[...] = jnp.zeros_like(part)
    for copy in local:
        copy.wait()
    for copy in arrivals:
        copy.wait_recv()

    def panel_of(p, cols):
        block = w_s[p, :, :, cols]
        if w_s.shape[2] % 16:
            block = block.astype(F32)
        return block.reshape(panel, block.shape[-1]).astype(BF16)

    @pl.loop(0, width // k_block)
    def _(i):
        cols = pl.ds(pl.multiple_of(i * k_block, k_block), k_block)
        v = v_s[:, :, cols].reshape(rows, k_block)
        first, second = panel_of(0, cols), panel_of(1, cols)
        part[:, :panel] += lax.dot_general(v, first, NT, preferred_element_type=F32)
        part[:, panel:2 * panel] += lax.dot_general(v, second, NT, preferred_element_type=F32)
        part[:, 2 * panel:] += lax.dot_general(first, second, NT, preferred_element_type=F32)

    rs_send[...] = part[...].astype(BF16).reshape(rs_send.shape)
    partners = [lax.rem(me_g + k, group) for k in range(1, group)]

    def place(g):
        return lax.rem(g, n_row), me_b * SPLIT + lax.div(g, n_row)

    got = []
    for g in partners:
        copy = remote(rs_send.at[g], rs_recv.at[me_g], r_send.at[g], r_recv.at[me_g], *place(g))
        copy.start()
        sends.append(copy)
        got.append(remote(rs_send.at[g], rs_recv.at[g], r_send.at[g], r_recv.at[g], *place(g)))
    total = rs_send[me_g].astype(F32)
    for g, copy in zip(partners, got):
        copy.wait_recv()
        total += rs_recv[g].astype(F32)
    ag[me_g] = total.astype(BF16)
    got = []
    for g in partners:
        copy = remote(ag.at[me_g], ag.at[me_g], g_send.at[g], g_recv.at[me_g], *place(g))
        copy.start()
        sends.append(copy)
        got.append(remote(ag.at[me_g], ag.at[g], g_send.at[g], g_recv.at[g], *place(g)))
    for copy in got:
        copy.wait_recv()

    sums = ag[...].reshape(rows, 3 * panel)
    high = lax.Precision.HIGHEST
    s1 = lax.dot_general(
        sums[:, :panel].astype(F32), t_ref[0], NT, precision=high, preferred_element_type=F32
    ).astype(BF16)
    p2 = sums[:, panel:2 * panel].astype(F32) - jnp.dot(
        s1, sums[:, 2 * panel:], preferred_element_type=F32
    )
    s2 = lax.dot_general(p2, t_ref[1], NT, precision=high, preferred_element_type=F32).astype(BF16)
    s_s[0] = s1
    s_s[1] = s2

    n_block = 2 * LANES
    got = []
    for j, (start, stop) in enumerate(out_blocks):
        size = min(stop, chunk) - start

        @pl.loop(start // n_block, stop // n_block)
        def _(i):
            cols = pl.ds(pl.multiple_of(i * n_block, n_block), n_block)
            v = v_s[:, :, cols].reshape(rows, n_block).astype(F32)
            v = v - jnp.dot(s_s[0], panel_of(0, cols), preferred_element_type=F32)
            v = v - jnp.dot(s_s[1], panel_of(1, cols), preferred_element_type=F32)
            v_s[:, :, cols] = v.astype(BF16).reshape(SPLIT, rows // SPLIT, n_block)

        def piece(g):
            r = lax.rem(g, n_row)
            return v_s.at[
                lax.div(g, n_row), pl.ds(pl.multiple_of(r * own, own), own), pl.ds(start, size)
            ]

        def landing(g):
            at = pl.multiple_of(lax.div(g, n_row) * chunk + start, LANES)
            return o_ref.at[lax.rem(g, n_row), :, pl.ds(at, size)]

        for g in partners:
            copy = remote(piece(g), landing(me_g), o_send.at[g, j], o_recv.at[me_g, j], *place(g))
            copy.start()
            sends.append(copy)
            got.append(remote(piece(g), landing(g), o_send.at[g, j], o_recv.at[g, j], *place(g)))
        copy = pltpu.make_async_copy(piece(me_g), landing(me_g), o_send.at[me_g, j])
        copy.start()
        got.append(copy)
    for copy in got:
        if hasattr(copy, "wait_recv") and copy.is_remote:
            copy.wait_recv()
        else:
            copy.wait()
    for copy in sends:
        copy.wait_send()


def shifted(x, offsets, mine, width):
    result = None
    for offset in sorted(set(offsets)):
        pads = [(0, 0)] * (x.ndim - 1) + [(offset, width - offset - x.shape[-1])]
        moved = jnp.pad(x, pads)
        result = moved if result is None else jnp.where(mine == offset, moved, result)
    return result


def assemble(received, columns):
    n_row = received.shape[0]
    pieces = []
    for r in range(n_row):
        low, high = r * columns, (r + 1) * columns
        first, last = low // LANES, -(-high // LANES)
        begin = 1 if low % LANES else 0
        shared = bool(high % LANES) and r + 1 < n_row
        end = last - first - (1 if shared else 0)
        stop = end * LANES if r + 1 < n_row else high - first * LANES
        pieces.append(received[r, :, begin * LANES:stop])
        if shared:
            pieces.append(
                received[r, :, end * LANES:(end + 1) * LANES] + received[r + 1, :, :LANES]
            )
    return jnp.concatenate(pieces, axis=1)


def body(n_row, n_col, vectors, reflectors, panel_factor):
    own_rows, columns = vectors.shape
    panel = panel_factor.shape[1]
    offsets = [r * columns % LANES for r in range(n_row)]
    chunk = -(-(columns + max(offsets)) // (SPLIT * LANES)) * LANES
    n_block = 2 * LANES
    width = -(-chunk // n_block) * n_block
    k_block = max(k for k in (256, 512, 768) if width % k == 0)
    mine = lax.axis_index("prow") * columns % LANES
    v = shifted(vectors, offsets, mine, SPLIT * chunk)
    w = shifted(reflectors, offsets, mine, SPLIT * chunk)
    group = SPLIT * n_row
    rows = SPLIT * own_rows
    step = -(-width // n_block // 4) * n_block
    out_blocks = [(s, min(s + step, width)) for s in range(0, width, step)]
    dma = pltpu.SemaphoreType.DMA
    received = pl.pallas_call(
        functools.partial(kernel, n_row, n_col, chunk, k_block, out_blocks),
        out_shape=jax.ShapeDtypeStruct((n_row, own_rows // n_row, SPLIT * chunk), BF16),
        in_specs=[
            pl.BlockSpec(memory_space=pl.ANY),
            pl.BlockSpec(memory_space=pl.ANY),
            pl.BlockSpec(memory_space=pltpu.VMEM),
        ],
        out_specs=pl.BlockSpec(memory_space=pl.ANY),
        scratch_shapes=[
            pltpu.VMEM((SPLIT, own_rows, width), BF16),
            pltpu.VMEM((2, n_col, reflectors.shape[1], width), BF16),
            pltpu.VMEM((rows, 3 * panel), F32),
            pltpu.VMEM((group, rows // group, 3 * panel), BF16),
            pltpu.VMEM((group, rows // group, 3 * panel), BF16),
            pltpu.VMEM((group, rows // group, 3 * panel), BF16),
            pltpu.VMEM((2, rows, panel), BF16),
            dma((SPLIT,)), dma((SPLIT,)), dma((n_col,)), dma((n_col,)),
            dma((group,)), dma((group,)), dma((group,)), dma((group,)),
            dma((group, len(out_blocks))), dma((group, len(out_blocks))), dma((2,)),
        ],
        compiler_params=pltpu.CompilerParams(
            has_side_effects=True, vmem_limit_bytes=56 * 1024 * 1024
        ),
        name="panels",
    )(v, w, panel_factor)
    return assemble(received, columns)[None]


def solution(mesh):
    placed = (P("pcol", "prow"), P(None, "pcol", "prow"), P())
    return jax.shard_map(
        functools.partial(body, mesh.shape["prow"], mesh.shape["pcol"]),
        mesh=mesh, in_specs=placed, out_specs=P("pcol", "prow", None), check_vma=False,
    )
```

time: 529 us -> 288 us (0.54)
  waiting for transfers between devices: 391 us -> 0 us
  Pallas kernels: 0 us -> 266 us
  blocking collectives: 68.6 us -> 0 us
  matrix products: 42.3 us -> 0 us
  between operations: 13.5 us -> 0.03 us
  other arithmetic: 0 us -> 11.6 us
  local copies, waits for them, and re-layouts: 13.8 us -> 6.92 us
    all_gather x2 -> x0, waiting for transfers between devices: 390 us -> none  [body(): single = lax.all_gather(reflectors[number], 'pcol', axis=0, tiled=True)]
    pallas_call x0 -> x1, Pallas kernels: none -> 266 us  [body(): pl.pallas_call(functools.partial(kernel, n_row, n_col, chunk, k_block, ou...]
    all_to_all x1 -> x0, blocking collectives: 47.1 us -> none  [body(): lax.all_to_all(current, 'prow', split_axis=0, concat_axis=1, tiled=True)]
    dot_general x6 -> x0, matrix products: 42.3 us -> none  [the longest x2 22.5 us: partial_products(): lax.dot_general(current, panel, (((1,), (1,)), ((), ())), preferred_eleme...]
    psum x2 -> x0, blocking collectives: 21.5 us -> none  [apply_panel(): lax.psum(partial_sum.astype(jnp.bfloat16), 'prow').astype(jnp.float32)]
    select_n x0 -> x2, other arithmetic: none -> 10.2 us  [shifted(): jnp.where(mine == offset, moved, result)]
    broadcast_in_dim x1 -> x0, local copies, waits for them, and re-layouts: 6.17 us -> none  [body(): return owned_rows[None]]
    unnamed x2 -> x7, local copies, waits for them, and re-layouts: 0.01 us -> 5.66 us
  transfers between devices with their start and end apart: 2 -> 0, of which waited for: 2 -> 0; matrix products, arithmetic and copies ran while one was open for 4% -> 0% of each run, Pallas kernels for 0% -> 0%
where the time goes in v1:
time: 288 us; the launch traced here: 285 us
  Pallas kernels  266 us (92%)
  other arithmetic  11.6 us (4%)
  local copies, waits for them, and re-layouts  6.92 us (2%)
    pallas_call x1, Pallas kernels, body(): pl.pallas_call(functools.partial(kernel, n_row, n_col, chunk, k_block, ou...  266 us
    select_n x2, other arithmetic, shifted(): jnp.where(mine == offset, moved, result)  10.2 us

profile of v1, /device:TPU:0, one launch (start us, length us, event | category | flops | bytes accessed | tf_op | source)
XLA Modules:
  0.0 284.7 jit_solution(4295855324715095693)
XLA Ops:
  0.0 0.0 copy-start
  0.0 6.8 %pad_select_fusion.1.v_ref = bf16[64,30208]{1,0:T(8,128)(2,1)} fusion(bf16[64,30016]{1,0:T(8,128)(2,1)} %param.3, pred[]{:T(512)S(6)} %eq.6), kind=kLoop, calls=%fused_computation.1 | loop fusion | flops 1933312 | bytes 7708673 | tf_op jit(solution)/shard_map/jit(_where)/select_n | solution.py:186
  6.8 0.0 copy-done
  6.8 3.4 %pad_select_fusion.w_ref = bf16[2,32,30208]{2,1,0:T(8,128)(2,1)} fusion(bf16[2,32,30016]{2,1,0:T(8,128)(2,1)S(1)} %copy-done, pred[]{:T(512)S(6)} %eq.6), kind=kLoop, calls=%fused_computation | loop fusion | flops 1933312 | bytes 7708673 | tf_op jit(solution)/shard_map/jit(_where)/select_n | solution.py:186
  10.2 266.2 %panels.1 = bf16[4,16,30208]{2,1,0:T(8,128)(2,1)} custom-call(bf16[64,30208]{1,0:T(8,128)(2,1)} %pad_select_fusion.1.v_ref, bf16[2,32,30208]{2,1,0:T(8,128)(2,1)} %pad_select_fusion.w_ref, f32[2,256,256]{2,1,0:T(8,128)} %t_ref.1), custom_call_target="tpu_custom_call" | custom-call | tf_op jit(solution)/shard_map/panels/pallas_call | solution.py:224
  276.4 1.3 bitcast_dynamic-update-slice_fusion.3
  277.7 0.7 constant_dynamic-update-slice_fusion.1
  278.4 1.3 bitcast_dynamic-update-slice_fusion.2
  279.6 1.3 bitcast_dynamic-update-slice_fusion.1
  280.9 0.7 constant_dynamic-update-slice_fusion
  281.6 1.3 bitcast_dynamic-update-slice_fusion
  282.8 0.0 copy-start.1
  282.9 1.9 copy-done.1
Async XLA Ops:
  0.0 6.8 %copy-start = (bf16[2,32,30016]{2,1,0:T(8,128)(2,1)S(1)}, bf16[2,32,30016]{2,1,0:T(8,128)(2,1)}, u32[]{:S(2)}) copy-start(bf16[2,32,30016]{2,1,0:T(8,128)(2,1)} %param.4) | copy-start | bytes 11526148
  282.8 1.9 copy-start.1

commit v2 on v1

v2 whole, which is shorter than its diff:
```python
import functools

import jax
import jax.numpy as jnp
from jax import lax
from jax.experimental import pallas as pl
from jax.experimental.pallas import tpu as pltpu
from jax.sharding import PartitionSpec as P

MESH = pl.DeviceIdType.MESH
LANES = 128
SPLIT = 4
F32, BF16 = jnp.float32, jnp.bfloat16
NT = (((1,), (1,)), ((), ()))


def kernel(
    n_row, n_col, main, k_block, out_blocks,
    v_ref, w_ref, vx_ref, wx_ref, t_ref, o_ref,
    v_s, w_s, part, rs_send, rs_recv, ag, s_s,
    v_send, v_recv, w_send, w_recv, r_send, r_recv, g_send, g_recv, o_send, o_recv, l_sem,
):
    me_r, me_c = lax.axis_index("prow"), lax.axis_index("pcol")
    me_a, me_b = lax.rem(me_c, SPLIT), lax.div(me_c, SPLIT)
    halves, group = n_col // SPLIT, SPLIT * n_row
    me_g = me_a * n_row + me_r
    width = v_s.shape[2]
    rows = SPLIT * v_s.shape[1]
    panel = w_s.shape[1] * w_s.shape[2]
    own = v_s.shape[1] // n_row
    middle = width // 2
    pieces = ((0, middle), (middle, main), (main, main + LANES))

    def remote(src, dst, send, recv, r, c):
        return pltpu.make_async_remote_copy(
            src_ref=src, dst_ref=dst, send_sem=send, recv_sem=recv,
            device_id={"prow": r, "pcol": c}, device_id_type=MESH,
        )

    def source(number, q):
        start, stop = pieces[number]
        if start == main:
            return pl.ds(pl.multiple_of(q * LANES, LANES), LANES)
        return pl.ds(pl.multiple_of(q * main + start, LANES), stop - start)

    def move(kind, number, b, q, c, here):
        start, stop = pieces[number]
        target = pl.ds(start, stop - start)
        if kind == "v":
            src = (vx_ref if start == main else v_ref).at[:, source(number, q)]
            slot, sent, come, mine, theirs = (
                lambda a: v_s.at[a, :, target], v_send, v_recv, me_a, q
            )
        else:
            src = (wx_ref if start == main else w_ref).at[:, :, source(number, q)]
            slot, sent, come, mine, theirs = (
                lambda a: w_s.at[:, a, :, target], w_send, w_recv, me_c, c
            )
        if here:
            copy = pltpu.make_async_copy(src, slot(mine), l_sem.at[number, 0 if kind == "v" else 1])
            copy.start()
            local[number].append(copy)
            return
        copy = remote(src, slot(mine), sent.at[number, theirs], come.at[number, mine], me_r, c)
        copy.start()
        sends.append(copy)
        arrivals[number].append(
            remote(src, slot(theirs), sent.at[number, theirs], come.at[number, theirs], me_r, c)
        )

    sends, arrivals, local = [], [[], [], []], [[], [], []]
    for number in (0, 2, 1):
        near, far = [], []
        for ka in reversed(range(SPLIT)):
            q = lax.rem(me_a + ka, SPLIT)
            near.append(("v", number, me_b, q, me_b * SPLIT + q, ka == 0))
            near.append(("w", number, me_b, q, me_b * SPLIT + q, ka == 0))
        for kb in reversed(range(1, halves)):
            b = lax.rem(me_b + kb, halves)
            for ka in reversed(range(SPLIT)):
                q = lax.rem(me_a + ka + 2 * me_r, SPLIT)
                far.append(("w", number, b, q, b * SPLIT + q, False))
        for at in range(max(len(near), len(far))):
            for order in (near, far):
                if at < len(order):
                    move(*order[at])
    if width > main + LANES:
        pad = width - main - LANES
        v_s[:, :, main + LANES:] = jnp.zeros((SPLIT, v_s.shape[1], pad), BF16)
        w_s[:, :, :, main + LANES:] = jnp.zeros((2, n_col, w_s.shape[2], pad), BF16)
    part[...] = jnp.zeros_like(part)

    def panel_of(p, cols):
        block = w_s[p, :, :, cols]
        if w_s.shape[2] % 16:
            block = block.astype(F32)
        return block.reshape(panel, block.shape[-1]).astype(BF16)

    def products(begin, end):
        @pl.loop(begin // k_block, end // k_block)
        def _(i):
            cols = pl.ds(pl.multiple_of(i * k_block, k_block), k_block)
            v = v_s[:, :, cols].reshape(rows, k_block)
            first, second = panel_of(0, cols), panel_of(1, cols)
            part[:, :panel] += lax.dot_general(v, first, NT, preferred_element_type=F32)
            part[:, panel:2 * panel] += lax.dot_general(v, second, NT, preferred_element_type=F32)
            part[:, 2 * panel:] += lax.dot_general(first, second, NT, preferred_element_type=F32)

    def landed(number):
        for copy in local[number]:
            copy.wait()
        for copy in arrivals[number]:
            copy.wait_recv()

    landed(0)
    products(0, middle)
    landed(2)
    landed(1)
    products(middle, width)

    rs_send[...] = part[...].astype(BF16).reshape(rs_send.shape)
    partners = [lax.rem(me_g + k, group) for k in range(1, group)]

    def place(g):
        return lax.rem(g, n_row), me_b * SPLIT + lax.div(g, n_row)

    got = []
    for g in partners:
        copy = remote(rs_send.at[g], rs_recv.at[me_g], r_send.at[g], r_recv.at[me_g], *place(g))
        copy.start()
        sends.append(copy)
        got.append(remote(rs_send.at[g], rs_recv.at[g], r_send.at[g], r_recv.at[g], *place(g)))
    total = rs_send[me_g].astype(F32)
    for g, copy in zip(partners, got):
        copy.wait_recv()
        total += rs_recv[g].astype(F32)
    ag[me_g] = total.astype(BF16)
    got = []
    for g in partners:
        copy = remote(ag.at[me_g], ag.at[me_g], g_send.at[g], g_recv.at[me_g], *place(g))
        copy.start()
        sends.append(copy)
        got.append(remote(ag.at[me_g], ag.at[g], g_send.at[g], g_recv.at[g], *place(g)))
    for copy in got:
        copy.wait_recv()

    sums = ag[...].reshape(rows, 3 * panel)
    high = lax.Precision.HIGHEST
    s1 = lax.dot_general(
        sums[:, :panel].astype(F32), t_ref[0], NT, precision=high, preferred_element_type=F32
    ).astype(BF16)
    p2 = sums[:, panel:2 * panel].astype(F32) - jnp.dot(
        s1, sums[:, 2 * panel:], preferred_element_type=F32
    )
    s2 = lax.dot_general(p2, t_ref[1], NT, precision=high, preferred_element_type=F32).astype(BF16)
    s_s[0] = s1
    s_s[1] = s2

    n_block = 2 * LANES
    got = []

    def hand_out(j, start, size):
        def piece(g):
            r = lax.rem(g, n_row)
            return v_s.at[
                lax.div(g, n_row), pl.ds(pl.multiple_of(r * own, own), own), pl.ds(start, size)
            ]

        def landing(g):
            a = lax.div(g, n_row)
            at = SPLIT * main + a * LANES if start == main else a * main + start
            return o_ref.at[lax.rem(g, n_row), :, pl.ds(pl.multiple_of(at, LANES), size)]

        for g in partners:
            copy = remote(piece(g), landing(me_g), o_send.at[g, j], o_recv.at[me_g, j], *place(g))
            copy.start()
            sends.append(copy)
            got.append(
                remote(piece(g), landing(g), o_send.at[g, j], o_recv.at[g, j], *place(g)).wait_recv
            )
        copy = pltpu.make_async_copy(piece(me_g), landing(me_g), o_send.at[me_g, j])
        copy.start()
        got.append(copy.wait)

    for j, (start, stop) in enumerate(out_blocks):

        @pl.loop(start // n_block, stop // n_block)
        def _(i):
            cols = pl.ds(pl.multiple_of(i * n_block, n_block), n_block)
            v = v_s[:, :, cols].reshape(rows, n_block).astype(F32)
            v = v - jnp.dot(s_s[0], panel_of(0, cols), preferred_element_type=F32)
            v = v - jnp.dot(s_s[1], panel_of(1, cols), preferred_element_type=F32)
            v_s[:, :, cols] = v.astype(BF16).reshape(SPLIT, rows // SPLIT, n_block)

        hand_out(j, start, min(stop, main) - start)
        if stop > main:
            hand_out(len(out_blocks), main, LANES)
    for wait in got:
        wait()
    for copy in sends:
        copy.wait_send()


def lay_out(columns, in_ref, out_ref):
    for r in range(in_ref.shape[0]):
        out_ref[:, r * columns:(r + 1) * columns] = in_ref[r, :, :columns]


def body(n_row, n_col, vectors, reflectors, panel_factor):
    own_rows, columns = vectors.shape
    panel = panel_factor.shape[1]
    main = columns // (SPLIT * LANES) * LANES
    covered = SPLIT * main
    k_block = 6 * LANES
    width = -(-(main + LANES) // (2 * k_block)) * 2 * k_block
    n_block = 2 * LANES
    extra = SPLIT * LANES - (columns - covered)
    v_x = jnp.pad(vectors[:, covered:], ((0, 0), (0, extra)))
    w_x = jnp.pad(reflectors[:, :, covered:], ((0, 0), (0, 0), (0, extra)))
    group = SPLIT * n_row
    rows = SPLIT * own_rows
    step = -(-width // n_block // 4) * n_block
    out_blocks = [(s, min(s + step, width)) for s in range(0, width, step)]
    out_count = len(out_blocks) + 1
    dma = pltpu.SemaphoreType.DMA
    received = pl.pallas_call(
        functools.partial(kernel, n_row, n_col, main, k_block, out_blocks),
        out_shape=jax.ShapeDtypeStruct(
            (n_row, own_rows // n_row, covered + SPLIT * LANES), BF16
        ),
        in_specs=[pl.BlockSpec(memory_space=pl.ANY)] * 4
        + [pl.BlockSpec(memory_space=pltpu.VMEM)],
        out_specs=pl.BlockSpec(memory_space=pl.ANY),
        scratch_shapes=[
            pltpu.VMEM((SPLIT, own_rows, width), BF16),
            pltpu.VMEM((2, n_col, reflectors.shape[1], width), BF16),
            pltpu.VMEM((rows, 3 * panel), F32),
            pltpu.VMEM((group, rows // group, 3 * panel), BF16),
            pltpu.VMEM((group, rows // group, 3 * panel), BF16),
            pltpu.VMEM((group, rows // group, 3 * panel), BF16),
            pltpu.VMEM((2, rows, panel), BF16),
            dma((3, SPLIT)), dma((3, SPLIT)), dma((3, n_col)), dma((3, n_col)),
            dma((group,)), dma((group,)), dma((group,)), dma((group,)),
            dma((group, out_count)), dma((group, out_count)), dma((3, 2)),
        ],
        compiler_params=pltpu.CompilerParams(
            has_side_effects=True, vmem_limit_bytes=56 * 1024 * 1024
        ),
        name="panels",
    )(vectors, reflectors, v_x, w_x, panel_factor)
    whole = pl.pallas_call(
        functools.partial(lay_out, columns),
        out_shape=jax.ShapeDtypeStruct((own_rows // n_row, n_row * columns), BF16),
        in_specs=[pl.BlockSpec(memory_space=pltpu.VMEM)],
        out_specs=pl.BlockSpec(memory_space=pltpu.VMEM),
        compiler_params=pltpu.CompilerParams(vmem_limit_bytes=24 * 1024 * 1024),
        name="lay_out",
    )(received)
    return whole[None]


def solution(mesh):
    placed = (P("pcol", "prow"), P(None, "pcol", "prow"), P())
    return jax.shard_map(
        functools.partial(body, mesh.shape["prow"], mesh.shape["pcol"]),
        mesh=mesh, in_specs=placed, out_specs=P("pcol", "prow", None), check_vma=False,
    )
```

time: 288 us -> 270 us (0.938)
  other arithmetic: 11.6 us -> 0 us
    select_n x2 -> x0, other arithmetic: 10.2 us -> none  [shifted(): jnp.where(mine == offset, moved, result)]
    unnamed x7 -> x2, local copies, waits for them, and re-layouts: 5.66 us -> 2.09 us
    pallas_call x1 -> x2, Pallas kernels: 266 us -> 264 us  [the longest x1 262 us: body(): pl.pallas_call(functools.partial(kernel, n_row, n_col, main, k_block, out...]
where the time goes in v2:
time: 270 us; the launch traced here: 269 us
  Pallas kernels  264 us (98%)
  local copies, waits for them, and re-layouts  4.95 us (2%)
    pallas_call x1, Pallas kernels, body(): pl.pallas_call(functools.partial(kernel, n_row, n_col, main, k_block, out...  262 us

profile of v2, /device:TPU:0, one launch (start us, length us, event | category | flops | bytes accessed | tf_op | source)
XLA Modules:
  0.0 269.0 jit_solution(3487421986352746510)
XLA Ops:
  0.0 0.8 slice.6
  0.8 0.6 pad.8.vx_ref
  1.4 0.8 slice.7
  2.2 0.6 pad.9.wx_ref
  2.9 261.5 %panels.1.in_ref = bf16[4,16,30208]{2,1,0:T(8,128)(2,1)} custom-call(bf16[64,30016]{1,0:T(8,128)(2,1)} %v_ref.1, bf16[2,32,30016]{2,1,0:T(8,128)(2,1)} %w_ref.1, bf16[64,512]{1,0:T(8,128)(2,1)} %pad.8.vx_ref, bf16[2,32,512]{2,1,0:T(8,128)(2,1)} %pad.9.wx_ref, f32[2,256,256]{2,1,0:T(8,128)} %t_ref.1), custom_call_target="tpu_custom_call" | custom-call | tf_op jit(solution)/shard_map/panels/pallas_call | solution.py:226
  264.4 0.0 copy-start
  264.4 2.1 copy-done
  266.5 2.5 lay_out.1
Async XLA Ops:
  264.4 2.1 copy-start

commit v3 on v2

--- a/solution.py
+++ b/solution.py
@@ -219,7 +219,7 @@
     w_x = jnp.pad(reflectors[:, :, covered:], ((0, 0), (0, 0), (0, extra)))
     group = SPLIT * n_row
     rows = SPLIT * own_rows
-    step = -(-width // n_block // 4) * n_block
+    step = -(-width // n_block // 6) * n_block
     out_blocks = [(s, min(s + step, width)) for s in range(0, width, step)]
     out_count = len(out_blocks) + 1
     dma = pltpu.SemaphoreType.DMA

time: 270 us -> 266 us (0.985)
  Pallas kernels: 264 us -> 261 us
    pallas_call x1, Pallas kernels: 262 us -> 258 us  [body(): pl.pallas_call(functools.partial(kernel, n_row, n_col, main, k_block, out...]
where the time goes in v3:
time: 266 us
  Pallas kernels  261 us (98%)
  local copies, waits for them, and re-layouts  4.95 us (2%)
    pallas_call x1, Pallas kernels, body(): pl.pallas_call(functools.partial(kernel, n_row, n_col, main, k_block, out...  258 us

profile of v3, /device:TPU:0, one launch (start us, length us, event | category | flops | bytes accessed | tf_op | source)
XLA Modules:
  0.0 265.6 jit_solution(4488055569958931962)
XLA Ops:
  0.0 0.8 slice.6
  0.8 0.6 pad.8.vx_ref
  1.4 0.8 slice.7
  2.2 0.6 pad.9.wx_ref
  2.9 258.2 %panels.1.in_ref = bf16[4,16,30208]{2,1,0:T(8,128)(2,1)} custom-call(bf16[64,30016]{1,0:T(8,128)(2,1)} %v_ref.1, bf16[2,32,30016]{2,1,0:T(8,128)(2,1)} %w_ref.1, bf16[64,512]{1,0:T(8,128)(2,1)} %pad.8.vx_ref, bf16[2,32,512]{2,1,0:T(8,128)(2,1)} %pad.9.wx_ref, f32[2,256,256]{2,1,0:T(8,128)} %t_ref.1), custom_call_target="tpu_custom_call" | custom-call | tf_op jit(solution)/shard_map/panels/pallas_call | solution.py:226
  261.0 0.0 copy-start
  261.0 2.1 copy-done
  263.1 2.5 lay_out.1
Async XLA Ops:
  261.0 2.1 copy-start
